TPU v7x, 128 devices: a whole 4x4x4 slice. The times are simulated.
128 devices in a mesh: dp: 8 (over z_hi, y), tensor: 16 (over x, z_lo, core).
Axes of the slice: x: 4, y: 4, z: 4 (z_hi: 2, z_lo: 2; z = z_hi * 2 + z_lo), core: 2. Of those that a mesh axis runs over, the one named last changes fastest.
Arguments:
- noisy: bfloat16 [64, 256, 1152], P('dp', None, 'tensor'), may hold values from -6 to 6
- labels: int32 [64], P('dp'), may hold values from 0 to 999
- tsteps: int32 [64], P('dp'), may hold values from 0 to 999
- guide_index: int32 [64], P('dp'), may hold values from 0 to 31
- class_table: bfloat16 [1001, 1152], replicated, may hold values from -6 to 6
- time_table: bfloat16 [1000, 1152], replicated, may hold values from -6 to 6
- guide_table: bfloat16 [32, 1152], replicated, may hold values from -6 to 6
- guide_weights: float32 [32], replicated, may hold values from 0.5 to 4
- teacher_qkv: bfloat16 [1152, 3456], P(None, 'tensor'), may hold values from -0.1875 to 0.1875
- teacher_out: bfloat16 [1152, 1152], P('tensor'), may hold values from -0.1875 to 0.1875
- teacher_ada: bfloat16 [3, 1152, 1152], P(None, None, 'tensor'), may hold values from -0.1875 to 0.1875
- student_qkv: bfloat16 [1152, 3456], P(None, 'tensor'), may hold values from -0.1875 to 0.1875
- student_out: bfloat16 [1152, 1152], P('tensor'), may hold values from -0.1875 to 0.1875
- student_ada: bfloat16 [3, 1152, 1152], P(None, None, 'tensor'), may hold values from -0.1875 to 0.1875
Outputs:
- grad_qkv: float32 [1152, 3456], P('dp', 'tensor')
- grad_out: float32 [1152, 1152], P('tensor', 'dp')
- grad_ada: float32 [3, 1152, 1152], P(None, 'dp', 'tensor')
All inputs are finite; a program needn't handle non-finite values.
Results may differ from a plain program's by a relative error of at most 0.034.
Values may be sent and summed in bfloat16 or wider, within the bound.
A program may use at most 128 MiB of HBM per device.

v0:
```python
import math
import jax
import jax.numpy as jnp
from jax import lax
from jax.sharding import PartitionSpec as P

HD = 72
norm_eps = 1e-06


def in_order(pieces, dim):
    shape = list(pieces.shape[1:])
    shape[dim] *= pieces.shape[0]
    return jnp.moveaxis(pieces, 0, dim).reshape(shape)


def sent_to_all(shard, axis):
    copies = jnp.broadcast_to(shard, (lax.axis_size(axis), *shard.shape))
    return lax.all_to_all(copies, axis, split_axis=0, concat_axis=0, tiled=True)


def collect(shard, axis, dim):
    return in_order(sent_to_all(shard, axis), dim)


def taken_together(shard, axis):
    return sent_to_all(shard, axis).sum(axis=0)


def in_one(arrays, axis):
    vector, at, outs = (jnp.concatenate([a.reshape(-1) for a in arrays]), 0, [])
    running = taken_together(vector, axis)
    for a in arrays:
        outs.append(running[at : at + a.size].reshape(a.shape))
        at += a.size
    return tuple(outs)


def in_blocks(shard, dim, devices):
    shape = shard.shape
    pieces = shard.reshape(*shape[:dim], devices, shape[dim] // devices, *shape[dim + 1 :])
    return jnp.moveaxis(pieces, dim, 0)


def sum_together(arrays, axis, dims):
    devices = lax.axis_size(axis)
    pieces = [in_blocks(a, dim, devices) for a, dim in zip(arrays, dims)]
    lines = jnp.concatenate([b.reshape(devices, -1) for b in pieces], axis=1)
    span = max(16, -(-lines.shape[1] // 1024) * 8)
    lines = jnp.pad(lines, ((0, 0), (0, span * 128 - lines.shape[1]))).reshape(-1, 128)
    vector, at, outs = (lax.psum_scatter(lines, axis, tiled=True).reshape(-1), 0, [])
    for b in pieces:
        part = b[0]
        outs.append(vector[at : at + part.size].reshape(part.shape))
        at += part.size
    return tuple(outs)


def lookup_rows(indices, table_rows):
    one_hot = (
        indices[:, None] == jnp.arange(table_rows.shape[0], dtype=jnp.int32)[None, :]
    ).astype(table_rows.dtype)
    return jnp.dot(one_hot, table_rows, preferred_element_type=jnp.float32)


def attend(qkv_sums, heads_here):
    batch_rows, seq_len = (qkv_sums.shape[0], qkv_sums.shape[1])
    heads_qkv = qkv_sums.astype(jnp.bfloat16).reshape(batch_rows, seq_len, heads_here, 3, HD)
    queries, key_rows, values = (
        heads_qkv[:, :, :, 0],
        heads_qkv[:, :, :, 1],
        heads_qkv[:, :, :, 2],
    )
    scores = jnp.einsum(
        "blhe,bmhe->bhlm", queries, key_rows, preferred_element_type=jnp.float32
    ) * (1.0 / math.sqrt(HD))
    exponent = jnp.exp(scores - jnp.max(scores, axis=-1, keepdims=True))
    attn_prob = exponent / jnp.sum(exponent, axis=-1, keepdims=True)
    prob_low = attn_prob.astype(jnp.bfloat16)
    attn_mixed = jnp.einsum("bhlm,bmhe->blhe", prob_low, values, preferred_element_type=jnp.float32)
    attn_mixed = attn_mixed.astype(jnp.bfloat16).reshape(batch_rows, seq_len, heads_here * HD)
    return (heads_qkv, attn_prob, prob_low, attn_mixed)


def attend_grad(heads_qkv, attn_prob, prob_low, grad_low):
    batch_rows, seq_len = (heads_qkv.shape[0], heads_qkv.shape[1])
    queries, key_rows, values = (
        heads_qkv[:, :, :, 0],
        heads_qkv[:, :, :, 1],
        heads_qkv[:, :, :, 2],
    )
    grad_probs = jnp.einsum("blhe,bmhe->bhlm", grad_low, values, preferred_element_type=jnp.float32)
    row_delta = jnp.sum(attn_prob * grad_probs, axis=-1, keepdims=True)
    grad_scores = (attn_prob * (grad_probs - row_delta) * (1.0 / math.sqrt(HD))).astype(
        jnp.bfloat16
    )
    grad_query = jnp.einsum(
        "bhlm,bmhe->blhe", grad_scores, key_rows, preferred_element_type=jnp.float32
    )
    grad_keys = jnp.einsum(
        "bhlm,blhe->bmhe", grad_scores, queries, preferred_element_type=jnp.float32
    )
    grad_values = jnp.einsum(
        "bhlm,blhe->bmhe", prob_low, grad_low, preferred_element_type=jnp.float32
    )
    grad_qkv_act = jnp.stack([grad_query, grad_keys, grad_values], axis=3).astype(jnp.bfloat16)
    return grad_qkv_act.reshape(batch_rows, seq_len, -1)


def forward(normed, wide_mod, qkv_weight, heads_here):
    full_rows = (
        normed.astype(jnp.float32) * (1.0 + wide_mod[:, 1][:, None]) + wide_mod[:, 0][:, None]
    ).astype(jnp.bfloat16)
    qkv_sums = jnp.einsum("bld,df->blf", full_rows, qkv_weight, preferred_element_type=jnp.float32)
    return attend(qkv_sums, heads_here)


def local(
    noisy,
    labels,
    tsteps,
    guide_index,
    class_table,
    time_table,
    guide_table,
    guide_weights,
    teacher_qkv,
    teacher_out,
    teacher_ada,
    student_qkv,
    student_out,
    student_ada,
):
    samples, seq_len, width_part = noisy.shape
    model_width = width_part * lax.axis_size("tensor")
    dp = lax.axis_size("dp")
    batch_size = samples * dp
    heads_here = student_out.shape[0] // HD
    wide = lax.all_gather(noisy, "tensor", axis=2, tiled=True)
    null_class = class_table.shape[0] - 1
    time_embed = lookup_rows(tsteps, time_table)
    cond_embed = lookup_rows(labels, class_table) + time_embed
    null_embed = class_table[null_class].astype(jnp.float32)[None, :] + time_embed
    guide_hot = guide_index[:, None] == jnp.arange(guide_table.shape[0], dtype=jnp.int32)[None, :]
    student_embed = cond_embed + jnp.dot(
        guide_hot.astype(jnp.bfloat16), guide_table, preferred_element_type=jnp.float32
    )
    strength = jnp.sum(jnp.where(guide_hot, guide_weights[None, :], 0.0), axis=1)
    cond_act = jax.nn.silu(cond_embed).astype(jnp.bfloat16)
    null_act = jax.nn.silu(null_embed).astype(jnp.bfloat16)
    student_act = jax.nn.silu(student_embed).astype(jnp.bfloat16)
    teacher_act = jnp.concatenate([cond_act, null_act], axis=0)
    mod_t = jnp.einsum("bd,kde->bke", teacher_act, teacher_ada, preferred_element_type=jnp.float32)
    mod_s = jnp.einsum("bd,kde->bke", student_act, student_ada, preferred_element_type=jnp.float32)
    wide_mod = collect(jnp.concatenate([mod_t, mod_s], axis=0), "tensor", 2)
    cond_mod, null_mod, student_mod = (
        wide_mod[:samples],
        wide_mod[samples : 2 * samples],
        wide_mod[2 * samples :],
    )
    scale_norm = 1.0 / math.sqrt(batch_size * seq_len)
    signal = wide.astype(jnp.float32)
    row_mean = jnp.sum(signal, axis=2) / model_width
    row_var = jnp.sum(signal * signal, axis=2) / model_width - row_mean * row_mean
    normed = ((signal - row_mean[:, :, None]) * lax.rsqrt(row_var + norm_eps)[:, :, None]).astype(
        jnp.bfloat16
    )
    teacher_mixed = forward(
        jnp.concatenate([normed, normed], axis=0), wide_mod[: 2 * samples], teacher_qkv, heads_here
    )[3]
    heads_qkv, attn_prob, prob_low, attn_mixed = forward(
        normed, student_mod, student_qkv, heads_here
    )
    teacher_part = jnp.einsum(
        "blf,fd->bld", teacher_mixed, teacher_out, preferred_element_type=jnp.float32
    )
    student_part = jnp.einsum(
        "blf,fd->bld", attn_mixed, student_out, preferred_element_type=jnp.float32
    )
    gate = student_mod[:, 2] * scale_norm
    cond_gate = (1.0 + strength)[:, None] * cond_mod[:, 2] * scale_norm
    null_gate = strength[:, None] * null_mod[:, 2] * scale_norm
    partial_cot = (
        gate[:, None] * student_part
        - cond_gate[:, None] * teacher_part[:samples]
        + null_gate[:, None] * teacher_part[samples:]
    )
    piece = lax.psum_scatter(
        partial_cot.astype(jnp.bfloat16), "tensor", scatter_dimension=2, tiled=True
    )
    cotangent = lax.all_gather(piece, "tensor", axis=2, tiled=True)
    grad_proj = (cotangent.astype(jnp.float32) * student_mod[:, 2][:, None]).astype(jnp.bfloat16)
    grad_mixed = jnp.einsum(
        "bld,ed->ble", grad_proj, student_out, preferred_element_type=jnp.float32
    )
    image_out = jnp.einsum(
        "ble,bld->bed", attn_mixed, cotangent, preferred_element_type=jnp.float32
    )
    grad_out_rows = jnp.sum(image_out * student_mod[:, 2][:, None], axis=0)
    grad_gate = jnp.sum(image_out * student_out.astype(jnp.float32)[None], axis=1)
    grad_low = grad_mixed.astype(jnp.bfloat16).reshape(samples, seq_len, heads_here, HD)
    grad_qkv_act = attend_grad(heads_qkv, attn_prob, prob_low, grad_low)
    image_qkv = jnp.einsum("bld,blf->bdf", normed, grad_qkv_act, preferred_element_type=jnp.float32)
    column_sums = jnp.sum(grad_qkv_act.astype(jnp.float32), axis=1)
    grad_qkv_local = jnp.sum(
        image_qkv * (1.0 + student_mod[:, 1])[:, :, None]
        + student_mod[:, 0][:, :, None] * column_sums[:, None, :],
        axis=0,
    )
    weight = student_qkv.astype(jnp.float32)
    grad_scale = jnp.sum(image_qkv * weight[None], axis=2)
    grad_shift = jnp.einsum("bf,df->bd", column_sums, weight, precision=lax.Precision.HIGHEST)
    grad_modulation = lax.psum_scatter(
        jnp.stack([grad_shift, grad_scale, grad_gate], axis=1),
        "tensor",
        scatter_dimension=2,
        tiled=True,
    )
    all_mod = lax.all_gather(grad_modulation, "dp", axis=0, tiled=True)
    act_rows = lax.all_to_all(student_act, "dp", split_axis=1, concat_axis=0, tiled=True)
    grad_ada = jnp.einsum(
        "bd,bke->kde", act_rows.astype(jnp.float32), all_mod, precision=lax.Precision.HIGHEST
    )
    grad_qkv = lax.psum_scatter(
        grad_qkv_local.astype(jnp.bfloat16), "dp", scatter_dimension=0, tiled=True
    ).astype(jnp.float32)
    grad_out = lax.psum_scatter(
        grad_out_rows.astype(jnp.bfloat16), "dp", scatter_dimension=1, tiled=True
    ).astype(jnp.float32)
    return (grad_qkv, grad_out, grad_ada)


def solution(mesh):
    return jax.shard_map(
        local,
        mesh=mesh,
        in_specs=(
            P("dp", None, "tensor"),
            P("dp"),
            P("dp"),
            P("dp"),
            P(),
            P(),
            P(),
            P(),
            P(None, "tensor"),
            P("tensor", None),
            P(None, None, "tensor"),
            P(None, "tensor"),
            P("tensor", None),
            P(None, None, "tensor"),
        ),
        out_specs=(P("dp", "tensor"), P("tensor", "dp"), P(None, "dp", "tensor")),
        check_vma=False,
    )
```

profile of v0, /device:TPU:0, one launch (start us, length us, event | category | flops | bytes accessed | tf_op | source)
XLA Modules:
  0.0 511.6 jit_solution(7823777829901788523)
XLA Ops:
  10.1 2.2 multiply_convert_fusion.7
  14.0 5.9 %all-to-all-start = ((f32[16,24,3,72]{3,1,2,0:T(8,128)}), f32[16,24,3,72]{3,1,2,0:T(8,128)S(1)}, u32[]{:S(2)}, u32[]{:S(2)}) async-start(f32[16,24,3,72]{3,1,2,0:T(8,128)} %broadcast_in_dim.10), calls=%async_computation | async-start | bytes 1179648 | tf_op jit(solution)/shard_map/all_to_all | solution.py:19
  20.1 14.4 %all-to-all-done = f32[16,24,3,72]{3,1,2,0:T(8,128)S(1)} async-done(((f32[16,24,3,72]{3,1,2,0:T(8,128)}), f32[16,24,3,72]{3,1,2,0:T(8,128)S(1)}, u32[]{:S(2)}, u32[]{:S(2)}) %all-to-all-start) | async-done | bytes 331808 | tf_op jit(solution)/shard_map/all_to_all | solution.py:19
  35.6 20.1 %all-gather.3.cloned.1.call-done = bf16[8,256,1152]{1,2,0:T(8,128)(2,1)} async-done(((bf16[8,256,72]{1,2,0:T(8,128)(2,1)}), bf16[8,256,1152]{1,2,0:T(8,128)(2,1)}) %all-gather.3.cloned.1.call-update) | async-done | bytes 4718608 | tf_op jit(solution)/shard_map/all_gather | solution.py:139
  55.7 3.7 convert_reduce_fusion
  60.6 9.5 %fusion.29 = bf16[16,256,216]{1,2,0:T(8,128)(2,1)S(1)} fusion(bf16[8,256,1152]{1,2,0:T(8,128)(2,1)S(1)} %fusion.4, f32[16,1152]{1,0:T(8,128)S(1)} %get-tuple-element.33, f32[16,1152]{1,0:T(8,128)S(1)} %get-tuple-element.32, bf16[1152,216]{0,1:T(8,128)(2,1)S(1)} %copy-done.11), kind=kOutput, calls=%fused_computation.49 | convolution fusion | flops 2062909440 | bytes 7133184 | tf_op jit(solution)/shard_map/bld,df->blf/dot_general | solution.py:114
  72.3 5.4 %fusion.36 = bf16[8,256,216]{1,2,0:T(8,128)(2,1)} fusion(bf16[8,256,1152]{1,2,0:T(8,128)(2,1)S(1)} %fusion.4, f32[8,1152]{1,0:T(8,128)S(1)} %get-tuple-element.36, f32[8,1152]{1,0:T(8,128)S(1)} %get-tuple-element.37, bf16[1152,216]{0,1:T(8,128)(2,1)S(1)} %copy-done.5), kind=kOutput, calls=%fused_computation.52 | convolution fusion | flops 1029095424 | bytes 6174720 | tf_op jit(solution)/shard_map/bld,df->blf/dot_general | solution.py:114
  77.7 3.3 fusion.98
  81.0 11.7 %fusion.39 = f32[16,256,1152]{1,2,0:T(8,128)} fusion(f32[16,256]{1,0:T(8,128)S(1)} %fusion.97, bf16[16,256,1,3,72]{1,4,3,0,2:T(8,128)(2,1)S(1)} %bitcast.190, f32[16,256,256]{1,2,0:T(8,128)} %copy-done.4, bf16[72,1152]{1,0:T(8,128)(2,1)S(1)} %copy-done.8), kind=kOutput, calls=%fused_computation.55 | convolution fusion | flops 836014336 | bytes 28035072 | tf_op jit(solution)/shard_map/blf,fd->bld/dot_general | solution.py:174
  92.7 2.1 fusion.47
  94.7 11.0 %fusion.99 = bf16[144,8,8,256]{3,1,0,2:T(8,128)(2,1)S(1)} fusion(f32[16,256,1152]{1,2,0:T(8,128)} %fusion.39, f32[8,1152]{1,0:T(8,128)S(1)} %fusion.69, f32[8,1152]{1,0:T(8,128)S(1)} %get-tuple-element.46, bf16[8,256,72]{1,2,0:T(8,128)(2,1)S(1)} %fusion.47, bf16[72,1152]{1,0:T(8,128)(2,1)S(1)} %copy-done.9, f32[8,1152]{1,0:T(8,128)S(1)} %get-tuple-element.35), kind=kOutput, calls=%fused_computation.135 | convolution fusion | flops 353894400 | bytes 24164352 | tf_op jit(solution)/shard_map/blf,fd->bld/dot_general | solution.py:177
  105.8 2.8 copy.180
  108.8 69.7 %reduce-scatter.11.cloned.1.call-done = bf16[72,2048]{1,0:T(8,128)(2,1)} async-done(((bf16[1152,2048]{1,0:T(8,128)(2,1)}), bf16[72,2048]{1,0:T(8,128)(2,1)}) %reduce-scatter.11.cloned.1.call-update) | async-done | bytes 294928
  181.5 35.3 %all-gather.5.cloned.1.call-done = bf16[8,256,1152]{1,2,0:T(8,128)(2,1)} async-done(((bf16[8,256,72]{1,2,0:T(8,128)(2,1)}), bf16[8,256,1152]{1,2,0:T(8,128)(2,1)}) %all-gather.5.cloned.1.call-update) | async-done | bytes 4718608 | tf_op jit(solution)/shard_map/all_gather | solution.py:191
  216.8 4.3 fusion.46
  221.1 2.1 convolution_bitcast_fusion.1
  224.6 3.8 fusion.43
  228.4 3.8 fusion.40
  234.2 6.2 %multiply_reduce_fusion = (f32[8,1152]{1,0:T(8,128)S(1)}, bf16[1152,216]{0,1:T(8,128)(2,1)S(1)}) fusion(f32[1152,216]{0,1:T(8,128)} %convert_element_type.156, f32[8,216]{1,0:T(8,128)S(1)} %mul.229, f32[8,1152]{1,0:T(8,128)S(1)} %get-tuple-element.36, f32[8,1152]{1,0:T(8,128)} %copy-done.10, bf16[8,256,1152]{1,2,0:T(8,128)(2,1)} %copy-done.3, ...), kind=kOutput, calls=%fused_computation.23 | convolution fusion | flops 1030901760 | bytes 7213824 | tf_op jit(solution)/shard_map/bld,blf->bdf/dot_general | solution.py:203
  245.7 6.9 %all-to-all-start.1 = ((bf16[8,8,144]{2,0,1:T(8,128)(2,1)}), bf16[8,8,144]{2,0,1:T(8,128)(2,1)S(1)}, u32[]{:S(2)}, u32[]{:S(2)}) async-start(bf16[8,8,144]{2,0,1:T(8,128)(2,1)} %copy.153), calls=%async_computation.1 | async-start | bytes 65536 | tf_op jit(solution)/shard_map/all_to_all | solution.py:220
  253.7 103.5 %all-reduce.3.cloned.1.call-done = f32[8,3,1152]{2,0,1:T(8,128)} async-done(((f32[8,3,1152]{2,0,1:T(8,128)}), f32[8,3,1152]{2,0,1:T(8,128)}) %all-reduce.3.cloned.1.call-update) | async-done | bytes 110608
  358.0 34.5 %all_gather.11 = f32[64,3,72]{2,0,1:T(8,128)S(1)} all-gather(f32[8,3,72]{2,0,1:T(8,128)S(1)} %constant_dynamic-slice_fusion), channel_id=1, replica_groups=mesh['dp'=8,'tensor'=16] {'dp'}, dimensions={0}, use_global_device_ids=true | all-gather | bytes 62208 | tf_op jit(solution)/shard_map/all_gather | solution.py:219
  393.6 34.5 %reduce-scatter.15.cloned.1.call-done = bf16[144,72]{1,0:T(8,128)(2,1)} async-done(((bf16[1152,72]{1,0:T(8,128)(2,1)}), bf16[144,72]{1,0:T(8,128)(2,1)}) %reduce-scatter.15.cloned.1.call-update) | async-done | bytes 20752
  429.6 73.3 %reduce-scatter.13.cloned.1.call-done = bf16[144,216]{1,0:T(8,128)(2,1)} async-done(((bf16[1152,216]{1,0:T(8,128)(2,1)}), bf16[144,216]{1,0:T(8,128)(2,1)}) %reduce-scatter.13.cloned.1.call-update) | async-done | bytes 62224
  (104 shorter events, 26.6 us)
Async XLA Ops:
  7.2 5.1 copy-start.12
  7.2 5.1 copy-start.13
  7.2 5.3 %copy-start.6 = (bf16[3,1152,72]{1,2,0:T(8,128)(2,1)S(1)}, bf16[3,1152,72]{1,2,0:T(8,128)(2,1)}, u32[]{:S(2)}) copy-start(bf16[3,1152,72]{1,2,0:T(8,128)(2,1)} %param.24) | copy-start | bytes 1492996
  7.2 5.6 %copy-start.7 = (bf16[3,1152,72]{1,2,0:T(8,128)(2,1)S(1)}, bf16[3,1152,72]{1,2,0:T(8,128)(2,1)}, u32[]{:S(2)}) copy-start(bf16[3,1152,72]{1,2,0:T(8,128)(2,1)} %param.27) | copy-start | bytes 1492996
  7.2 12.7 %copy-start.14 = (f32[32]{0:T(128)S(1)}, f32[32]{0:T(128)}, u32[]{:S(2)}) copy-start(f32[32]{0:T(128)} %param.21) | copy-start | bytes 388
  7.2 48.5 %all-gather.3.cloned.1.call-start = ((), (), s32[]{:S(2)}) async-start(), calls=%async_computation.5 | async-start | bytes 5013504 | tf_op jit(solution)/shard_map/all_gather | solution.py:139
  14.0 20.5 %all-to-all-start = ((f32[16,24,3,72]{3,1,2,0:T(8,128)}), f32[16,24,3,72]{3,1,2,0:T(8,128)S(1)}, u32[]{:S(2)}, u32[]{:S(2)}) async-start(f32[16,24,3,72]{3,1,2,0:T(8,128)} %broadcast_in_dim.10), calls=%async_computation | async-start | bytes 1179648 | tf_op jit(solution)/shard_map/all_to_all | solution.py:19
  19.9 158.7 %reduce-scatter.11.cloned.1.call-start = ((), (), s32[]{:S(2)}) async-start(), calls=%async_computation.7 | async-start | bytes 5013504
  35.6 36.4 %copy-start.10 = (f32[8,1152]{1,0:T(8,128)}, f32[8,1152]{1,0:T(8,128)S(1)}, u32[]{:S(2)}) copy-start(f32[8,1152]{1,0:T(8,128)S(1)} %get-tuple-element.37) | copy-start | bytes 110596
  55.7 3.8 copy-start.2
  60.6 11.4 %copy-start.3 = (bf16[8,256,1152]{1,2,0:T(8,128)(2,1)}, bf16[8,256,1152]{1,2,0:T(8,128)(2,1)S(1)}, u32[]{:S(2)}) copy-start(bf16[8,256,1152]{1,2,0:T(8,128)(2,1)S(1)} %fusion.4) | copy-start | bytes 14155780
  70.9 6.8 %copy-start.4 = (f32[16,256,256]{1,2,0:T(8,128)}, f32[16,256,256]{1,2,0:T(8,128)S(1)}, u32[]{:S(2)}) copy-start(f32[16,256,256]{1,2,0:T(8,128)S(1)} %fusion.51) | copy-start | bytes 12582916
  72.3 8.7 %copy-start.8 = (bf16[72,1152]{1,0:T(8,128)(2,1)S(1)}, bf16[72,1152]{1,0:T(8,128)(2,1)}, u32[]{:S(2)}) copy-start(bf16[72,1152]{1,0:T(8,128)(2,1)} %param.23) | copy-start | bytes 497668
  94.7 11.0 %copy-start.16 = (bf16[8,256,72]{1,2,0:T(8,128)(2,1)}, bf16[8,256,72]{1,2,0:T(8,128)(2,1)S(1)}, u32[]{:S(2)}) copy-start(bf16[8,256,72]{1,2,0:T(8,128)(2,1)S(1)} %fusion.47) | copy-start | bytes 884740
  108.6 108.2 %all-gather.5.cloned.1.call-start = ((), (), s32[]{:S(2)}) async-start(), calls=%async_computation.6 | async-start | bytes 5013504 | tf_op jit(solution)/shard_map/all_gather | solution.py:191
  180.4 176.9 %all-reduce.3.cloned.1.call-start = ((), (), s32[]{:S(2)}) async-start(), calls=%async_computation.10 | async-start | bytes 221184
  233.8 6.7 %slice-start = ((s8[4718592]{0:T(1024)(128)(4,1)}), s8[4194304]{0:T(1024)(128)(4,1)S(1)}, s32[]{:S(2)}) async-start(s8[4718592]{0:T(1024)(128)(4,1)} %bitcast.203), calls=%async_computation.11 | async-start | bytes 8388608
  234.2 6.3 %slice-start.1 = ((s8[4718592]{0:T(1024)(128)(4,1)}), s8[524288]{0:T(1024)(128)(4,1)S(1)}, s32[]{:S(2)}) async-start(s8[4718592]{0:T(1024)(128)(4,1)} %bitcast.203), calls=%async_computation.12 | async-start | bytes 1048576
  234.2 6.3 %copy-start.17 = (bf16[8,256,72]{1,2,0:T(8,128)(2,1)S(1)}, bf16[8,256,72]{1,2,0:T(8,128)(2,1)}, u32[]{:S(2)}) copy-start(bf16[8,256,72]{1,2,0:T(8,128)(2,1)} %copy-done.16) | copy-start | bytes 884740
  234.2 270.5 %copy-start.1 = (bf16[1000,1152]{1,0:T(8,128)(2,1)S(1)}, bf16[1000,1152]{1,0:T(8,128)(2,1)}, u32[]{:S(2)}) copy-start(bf16[1000,1152]{1,0:T(8,128)(2,1)} %param.19) | copy-start | bytes 6912004
  240.5 12.0 %copy-start.15 = (u32[128]{0:T(128)S(1)}, u32[128]{0:T(128)}, u32[]{:S(2)}) copy-start(u32[128]{0:T(128)} %constant.33) | copy-start | bytes 1540
  242.8 185.3 %reduce-scatter.15.cloned.1.call-start = ((), (), s32[]{:S(2)}) async-start(), calls=%async_computation.9 | async-start | bytes 331776
  243.8 259.2 %reduce-scatter.13.cloned.1.call-start = ((), (), s32[]{:S(2)}) async-start(), calls=%async_computation.8 | async-start | bytes 663552
  245.7 146.8 %all-to-all-start.1 = ((bf16[8,8,144]{2,0,1:T(8,128)(2,1)}), bf16[8,8,144]{2,0,1:T(8,128)(2,1)S(1)}, u32[]{:S(2)}, u32[]{:S(2)}) async-start(bf16[8,8,144]{2,0,1:T(8,128)(2,1)} %copy.153), calls=%async_computation.1 | async-start | bytes 65536 | tf_op jit(solution)/shard_map/all_to_all | solution.py:220
  (4 other events, 6.4 us)
Sparse Core Ops, SparseCore 0:
  9.7 45.9 all-gather.2
  108.7 69.8 reduce-scatter.10
  180.5 36.2 all-gather.4
  242.9 114.2 all-reduce.2
  360.7 67.4 reduce-scatter.14
  431.6 71.3 reduce-scatter.12
where the time goes:
time: 512 us
  waiting for transfers between devices  352 us (69%)
  matrix products  71.6 us (14%)
  blocking collectives  34.5 us (7%)
  between operations  15.1 us (3%)
  local copies, waits for them, and re-layouts  14.4 us (3%)
  starting transfers between devices  13.1 us (3%)
  other arithmetic  11.2 us (2%)
    unnamed x10, waiting for transfers between devices  282 us
    all_gather x1, waiting for transfers between devices, local(): cotangent = lax.all_gather(piece, 'tensor', axis=2, tiled=True)  35.3 us
    all_gather x1, blocking collectives, local(): all_mod = lax.all_gather(grad_modulation, 'dp', axis=0, tiled=True)  34.5 us
    all_gather x1, waiting for transfers between devices, local(): wide = lax.all_gather(noisy, 'tensor', axis=2, tiled=True)  20.1 us
    dot_general x2, matrix products, forward(): jnp.einsum('bld,df->blf', full_rows, qkv_weight, preferred_element_type=j...  14.9 us
    all_to_all x1, waiting for transfers between devices, sent_to_all(): return lax.all_to_all(copies, axis, split_axis=0, concat_axis=0, tiled=True)  14.4 us
    unnamed x51, local copies, waits for them, and re-layouts  11.8 us
    dot_general x1, matrix products, local(): jnp.einsum('blf,fd->bld', teacher_mixed, teacher_out, preferred_element_t...  11.7 us
  transfers between devices with their start and end apart: 8, of which 7 were waited for; matrix products, arithmetic and copies ran while one was open for 3% of the time, Pallas kernels for 0%

commit v1 on v0

--- a/solution.py
+++ b/solution.py
@@ -188,7 +188,7 @@
     piece = lax.psum_scatter(
         partial_cot.astype(jnp.bfloat16), "tensor", scatter_dimension=2, tiled=True
     )
-    cotangent = lax.all_gather(piece, "tensor", axis=2, tiled=True)
+    cotangent = jnp.concatenate(lax.all_gather(piece, "tensor"), axis=2)
     grad_proj = (cotangent.astype(jnp.float32) * student_mod[:, 2][:, None]).astype(jnp.bfloat16)
     grad_mixed = jnp.einsum(
         "bld,ed->ble", grad_proj, student_out, preferred_element_type=jnp.float32

time: 512 us -> 515 us (level)
    unnamed x51 -> x47, local copies, waits for them, and re-layouts: 11.8 us -> 12.6 us
where the time goes in v1:
time: 515 us; the launch traced here: 514 us
  waiting for transfers between devices  352 us (68%)
  matrix products  70.3 us (14%)
  blocking collectives  34.5 us (7%)
  local copies, waits for them, and re-layouts  17.9 us (3%)
  between operations  15.1 us (3%)
  starting transfers between devices  13.1 us (3%)
  other arithmetic  11.2 us (2%)
    unnamed x10, waiting for transfers between devices  282 us
    all_gather x1, waiting for transfers between devices, local(): cotangent = jnp.concatenate(lax.all_gather(piece, 'tensor'), axis=2)  35.4 us
    all_gather x1, blocking collectives, local(): all_mod = lax.all_gather(grad_modulation, 'dp', axis=0, tiled=True)  34.5 us
    all_gather x1, waiting for transfers between devices, local(): wide = lax.all_gather(noisy, 'tensor', axis=2, tiled=True)  20.1 us
    dot_general x2, matrix products, forward(): jnp.einsum('bld,df->blf', full_rows, qkv_weight, preferred_element_type=j...  14.9 us
    all_to_all x1, waiting for transfers between devices, sent_to_all(): return lax.all_to_all(copies, axis, split_axis=0, concat_axis=0, tiled=True)  14.4 us
    unnamed x47, local copies, waits for them, and re-layouts  12.6 us
    dot_general x1, matrix products, local(): jnp.einsum('blf,fd->bld', teacher_mixed, teacher_out, preferred_element_t...  11.7 us
  transfers between devices with their start and end apart: 8, of which 7 were waited for; matrix products, arithmetic and copies ran while one was open for 3% of the time, Pallas kernels for 0%

profile of v1, /device:TPU:0, one launch (start us, length us, event | category | flops | bytes accessed | tf_op | source)
XLA Modules:
  0.0 513.7 jit_solution(9893021585539589534)
XLA Ops:
  10.1 2.2 multiply_convert_fusion.7
  14.0 5.9 %all-to-all-start = ((f32[16,24,3,72]{3,1,2,0:T(8,128)}), f32[16,24,3,72]{3,1,2,0:T(8,128)S(1)}, u32[]{:S(2)}, u32[]{:S(2)}) async-start(f32[16,24,3,72]{3,1,2,0:T(8,128)} %broadcast_in_dim.10), calls=%async_computation | async-start | bytes 1179648 | tf_op jit(solution)/shard_map/all_to_all | solution.py:19
  20.1 14.4 %all-to-all-done = f32[16,24,3,72]{3,1,2,0:T(8,128)S(1)} async-done(((f32[16,24,3,72]{3,1,2,0:T(8,128)}), f32[16,24,3,72]{3,1,2,0:T(8,128)S(1)}, u32[]{:S(2)}, u32[]{:S(2)}) %all-to-all-start) | async-done | bytes 331808 | tf_op jit(solution)/shard_map/all_to_all | solution.py:19
  35.6 20.1 %all-gather.4.cloned.1.call-done = bf16[8,256,1152]{1,2,0:T(8,128)(2,1)} async-done(((bf16[8,256,72]{1,2,0:T(8,128)(2,1)}), bf16[8,256,1152]{1,2,0:T(8,128)(2,1)}) %all-gather.4.cloned.1.call-update) | async-done | bytes 4718608 | tf_op jit(solution)/shard_map/all_gather | solution.py:139
  55.7 3.7 convert_reduce_fusion
  60.6 9.5 %fusion.29 = bf16[16,256,216]{1,2,0:T(8,128)(2,1)S(1)} fusion(bf16[8,256,1152]{1,2,0:T(8,128)(2,1)S(1)} %fusion.4, f32[16,1152]{1,0:T(8,128)S(1)} %get-tuple-element.33, f32[16,1152]{1,0:T(8,128)S(1)} %get-tuple-element.32, bf16[1152,216]{0,1:T(8,128)(2,1)S(1)} %copy-done.11), kind=kOutput, calls=%fused_computation.49 | convolution fusion | flops 2062909440 | bytes 7133184 | tf_op jit(solution)/shard_map/bld,df->blf/dot_general | solution.py:114
  72.3 5.4 %fusion.36 = bf16[8,256,216]{1,2,0:T(8,128)(2,1)} fusion(bf16[8,256,1152]{1,2,0:T(8,128)(2,1)S(1)} %fusion.4, f32[8,1152]{1,0:T(8,128)S(1)} %get-tuple-element.36, f32[8,1152]{1,0:T(8,128)S(1)} %get-tuple-element.37, bf16[1152,216]{0,1:T(8,128)(2,1)S(1)} %copy-done.6), kind=kOutput, calls=%fused_computation.52 | convolution fusion | flops 1029095424 | bytes 6174720 | tf_op jit(solution)/shard_map/bld,df->blf/dot_general | solution.py:114
  77.7 3.2 fusion.98
  81.0 11.7 %fusion.39 = f32[16,256,1152]{1,2,0:T(8,128)} fusion(f32[16,256]{1,0:T(8,128)S(1)} %fusion.97, bf16[16,256,1,3,72]{1,4,3,0,2:T(8,128)(2,1)S(1)} %bitcast.197, f32[16,256,256]{1,2,0:T(8,128)} %copy-done.5, bf16[72,1152]{1,0:T(8,128)(2,1)S(1)} %copy-done.9), kind=kOutput, calls=%fused_computation.55 | convolution fusion | flops 836014336 | bytes 28035072 | tf_op jit(solution)/shard_map/blf,fd->bld/dot_general | solution.py:174
  94.7 11.0 %fusion.99 = bf16[144,8,8,256]{3,1,0,2:T(8,128)(2,1)S(1)} fusion(f32[16,256,1152]{1,2,0:T(8,128)} %fusion.39, f32[8,1152]{1,0:T(8,128)S(1)} %fusion.69, f32[8,1152]{1,0:T(8,128)S(1)} %get-tuple-element.46, bf16[8,256,72]{1,2,0:T(8,128)(2,1)S(1)} %fusion.47, bf16[72,1152]{1,0:T(8,128)(2,1)S(1)} %copy-done.10, f32[8,1152]{1,0:T(8,128)S(1)} %get-tuple-element.35), kind=kOutput, calls=%fused_computation.135 | convolution fusion | flops 353894400 | bytes 24164352 | tf_op jit(solution)/shard_map/blf,fd->bld/dot_general | solution.py:177
  105.8 2.8 copy.190
  108.8 69.7 %reduce-scatter.11.cloned.1.call-done = bf16[72,2048]{1,0:T(8,128)(2,1)} async-done(((bf16[1152,2048]{1,0:T(8,128)(2,1)}), bf16[72,2048]{1,0:T(8,128)(2,1)}) %reduce-scatter.11.cloned.1.call-update) | async-done | bytes 294928
  181.4 35.4 %all-gather.6.cloned.1.call-done = bf16[128,256,72]{1,2,0:T(8,128)(2,1)} async-done(((bf16[8,256,72]{1,2,0:T(8,128)(2,1)}), bf16[128,256,72]{1,2,0:T(8,128)(2,1)}) %all-gather.6.cloned.1.call-update) | async-done | bytes 4718608 | tf_op jit(solution)/shard_map/all_gather | solution.py:191
  216.8 2.6 copy.153
  219.5 2.3 fusion.46
  224.5 3.8 fusion.43
  228.4 3.8 fusion.40
  233.8 4.0 multiply_reduce_fusion.2
  238.2 6.1 %multiply_reduce_fusion = (f32[8,1152]{1,0:T(8,128)S(1)}, bf16[1152,216]{0,1:T(8,128)(2,1)S(1)}) fusion(f32[1152,216]{0,1:T(8,128)} %convert_element_type.156, f32[8,216]{1,0:T(8,128)S(1)} %mul.229, f32[8,1152]{1,0:T(8,128)S(1)} %get-tuple-element.36, f32[8,1152]{1,0:T(8,128)S(1)} %get-tuple-element.37, bf16[8,256,1152]{1,2,0:T(8,128)(2,1)} %copy-done.3, ...), kind=kOutput, calls=%fused_computation.23 | convolution fusion | flops 1030901760 | bytes 7213824 | tf_op jit(solution)/shard_map/bld,blf->bdf/dot_general | solution.py:203
  247.8 6.8 %all-to-all-start.1 = ((bf16[8,8,144]{2,0,1:T(8,128)(2,1)}), bf16[8,8,144]{2,0,1:T(8,128)(2,1)S(1)}, u32[]{:S(2)}, u32[]{:S(2)}) async-start(bf16[8,8,144]{2,0,1:T(8,128)(2,1)} %copy.162), calls=%async_computation.1 | async-start | bytes 65536 | tf_op jit(solution)/shard_map/all_to_all | solution.py:220
  255.9 103.5 %all-reduce.3.cloned.1.call-done = f32[8,3,1152]{2,0,1:T(8,128)} async-done(((f32[8,3,1152]{2,0,1:T(8,128)}), f32[8,3,1152]{2,0,1:T(8,128)}) %all-reduce.3.cloned.1.call-update) | async-done | bytes 110608
  360.2 34.5 %all_gather.15 = f32[64,3,72]{2,0,1:T(8,128)S(1)} all-gather(f32[8,3,72]{2,0,1:T(8,128)S(1)} %constant_dynamic-slice_fusion), channel_id=1, replica_groups=mesh['dp'=8,'tensor'=16] {'dp'}, dimensions={0}, use_global_device_ids=true | all-gather | bytes 62208 | tf_op jit(solution)/shard_map/all_gather | solution.py:219
  395.8 34.5 %reduce-scatter.15.cloned.1.call-done = bf16[144,72]{1,0:T(8,128)(2,1)} async-done(((bf16[1152,72]{1,0:T(8,128)(2,1)}), bf16[144,72]{1,0:T(8,128)(2,1)}) %reduce-scatter.15.cloned.1.call-update) | async-done | bytes 20752
  431.8 73.3 %reduce-scatter.13.cloned.1.call-done = bf16[144,216]{1,0:T(8,128)(2,1)} async-done(((bf16[1152,216]{1,0:T(8,128)(2,1)}), bf16[144,216]{1,0:T(8,128)(2,1)}) %reduce-scatter.13.cloned.1.call-update) | async-done | bytes 62224
  (100 shorter events, 28.4 us)
Async XLA Ops:
  7.2 1.8 copy-start
  7.2 5.1 copy-start.12
  7.2 5.1 copy-start.13
  7.2 5.3 %copy-start.7 = (bf16[3,1152,72]{1,2,0:T(8,128)(2,1)S(1)}, bf16[3,1152,72]{1,2,0:T(8,128)(2,1)}, u32[]{:S(2)}) copy-start(bf16[3,1152,72]{1,2,0:T(8,128)(2,1)} %param.24) | copy-start | bytes 1492996
  7.2 5.6 %copy-start.8 = (bf16[3,1152,72]{1,2,0:T(8,128)(2,1)S(1)}, bf16[3,1152,72]{1,2,0:T(8,128)(2,1)}, u32[]{:S(2)}) copy-start(bf16[3,1152,72]{1,2,0:T(8,128)(2,1)} %param.27) | copy-start | bytes 1492996
  7.2 12.7 %copy-start.14 = (f32[32]{0:T(128)S(1)}, f32[32]{0:T(128)}, u32[]{:S(2)}) copy-start(f32[32]{0:T(128)} %param.21) | copy-start | bytes 388
  7.2 48.5 %all-gather.4.cloned.1.call-start = ((), (), s32[]{:S(2)}) async-start(), calls=%async_computation.5 | async-start | bytes 5013504 | tf_op jit(solution)/shard_map/all_gather | solution.py:139
  14.0 20.5 %all-to-all-start = ((f32[16,24,3,72]{3,1,2,0:T(8,128)}), f32[16,24,3,72]{3,1,2,0:T(8,128)S(1)}, u32[]{:S(2)}, u32[]{:S(2)}) async-start(f32[16,24,3,72]{3,1,2,0:T(8,128)} %broadcast_in_dim.10), calls=%async_computation | async-start | bytes 1179648 | tf_op jit(solution)/shard_map/all_to_all | solution.py:19
  19.9 158.6 %reduce-scatter.11.cloned.1.call-start = ((), (), s32[]{:S(2)}) async-start(), calls=%async_computation.7 | async-start | bytes 5013504
  55.7 3.8 copy-start.2
  60.6 11.3 %copy-start.3 = (bf16[8,256,1152]{1,2,0:T(8,128)(2,1)}, bf16[8,256,1152]{1,2,0:T(8,128)(2,1)S(1)}, u32[]{:S(2)}) copy-start(bf16[8,256,1152]{1,2,0:T(8,128)(2,1)S(1)} %fusion.4) | copy-start | bytes 14155780
  70.9 6.8 %copy-start.5 = (f32[16,256,256]{1,2,0:T(8,128)}, f32[16,256,256]{1,2,0:T(8,128)S(1)}, u32[]{:S(2)}) copy-start(f32[16,256,256]{1,2,0:T(8,128)S(1)} %fusion.51) | copy-start | bytes 12582916
  72.3 8.7 %copy-start.9 = (bf16[72,1152]{1,0:T(8,128)(2,1)S(1)}, bf16[72,1152]{1,0:T(8,128)(2,1)}, u32[]{:S(2)}) copy-start(bf16[72,1152]{1,0:T(8,128)(2,1)} %param.23) | copy-start | bytes 497668
  92.7 2.1 copy-start.10
  94.7 11.0 %copy-start.16 = (bf16[8,256,72]{1,2,0:T(8,128)(2,1)}, bf16[8,256,72]{1,2,0:T(8,128)(2,1)S(1)}, u32[]{:S(2)}) copy-start(bf16[8,256,72]{1,2,0:T(8,128)(2,1)S(1)} %fusion.47) | copy-start | bytes 884740
  108.6 108.2 %all-gather.6.cloned.1.call-start = ((), (), s32[]{:S(2)}) async-start(), calls=%async_computation.6 | async-start | bytes 5013504 | tf_op jit(solution)/shard_map/all_gather | solution.py:191
  180.3 179.1 %all-reduce.3.cloned.1.call-start = ((), (), s32[]{:S(2)}) async-start(), calls=%async_computation.10 | async-start | bytes 221184
  219.5 3.6 copy-start.4
  219.5 3.2 copy-start.17
  238.2 16.4 %copy-start.15 = (u32[128]{0:T(128)S(1)}, u32[128]{0:T(128)}, u32[]{:S(2)}) copy-start(u32[128]{0:T(128)} %constant.33) | copy-start | bytes 1540
  238.2 268.6 %copy-start.1 = (bf16[1000,1152]{1,0:T(8,128)(2,1)S(1)}, bf16[1000,1152]{1,0:T(8,128)(2,1)}, u32[]{:S(2)}) copy-start(bf16[1000,1152]{1,0:T(8,128)(2,1)} %param.19) | copy-start | bytes 6912004
  245.0 185.3 %reduce-scatter.15.cloned.1.call-start = ((), (), s32[]{:S(2)}) async-start(), calls=%async_computation.9 | async-start | bytes 331776
  246.0 259.1 %reduce-scatter.13.cloned.1.call-start = ((), (), s32[]{:S(2)}) async-start(), calls=%async_computation.8 | async-start | bytes 663552
  247.8 146.8 %all-to-all-start.1 = ((bf16[8,8,144]{2,0,1:T(8,128)(2,1)}), bf16[8,8,144]{2,0,1:T(8,128)(2,1)S(1)}, u32[]{:S(2)}, u32[]{:S(2)}) async-start(bf16[8,8,144]{2,0,1:T(8,128)(2,1)} %copy.162), calls=%async_computation.1 | async-start | bytes 65536 | tf_op jit(solution)/shard_map/all_to_all | solution.py:220
  (2 other events, 2.6 us)
Sparse Core Ops, SparseCore 0:
  9.7 45.9 all-gather.3
  108.7 69.7 reduce-scatter.10
  180.4 36.3 all-gather.5
  245.1 114.1 all-reduce.2
  362.8 67.4 reduce-scatter.14
  433.7 71.3 reduce-scatter.12
